TPU v7x, 32 devices: a whole 2x2x4 slice. The times are simulated.
32 devices in a mesh: dp: 8 (over y, x, core), mp: 4 (over z).
Axes of the slice: x: 2, y: 2, z: 4, core: 2. Of those that a mesh axis runs over, the one named last changes fastest.
Arguments:
- tokens: bfloat16 [16384, 1024], P(('dp', 'mp')), may hold values from -6 to 6
- norm_gain: float32 [2, 1024], replicated, may hold values from 0.1 to 1.9
- qkv_weight: bfloat16 [3, 1024, 1024], P(None, 'dp', 'mp')
- out_weight: bfloat16 [1024, 1024], P('mp', 'dp'), may hold values from -0.1875 to 0.1875
- variate_bias: float32 [2, 16], replicated, may hold values from -6 to 6
- ffn_weight: bfloat16 [2, 1024, 2816], P(None, 'dp', 'mp'), may hold values from -0.1875 to 0.1875
- down_weight: bfloat16 [2816, 1024], P('mp', 'dp'), may hold values from -0.109375 to 0.109375
- sample_ids: int32 [16384], P(('dp', 'mp')), may hold values from 0 to 127, as said below
- variate_ids: int32 [16384], P(('dp', 'mp')), may hold values from 0 to 15, as said below
- time_ids: int32 [16384], P(('dp', 'mp')), may hold values from 0 to 31, as said below
Outputs:
- encoded: bfloat16 [16384, 1024], P(('dp', 'mp'))
Inputs may be any that keep to these rules, and one draw needn't show every extreme that they name: `sample_ids`: within each packed sequence of 512 tokens the series numbers start at 0 and never fall; a series with v variates (1 to 16) and p patches (4 to 32) holds v * p consecutive tokens, the last series of a sequence may be cut short; some packed sequence holds 128 series of one variate and four patches each. `variate_ids`: A token's offset within its series divided by that series' patch count p. `time_ids`: A token's offset within its series modulo that series' patch count p.
All inputs are finite; a program needn't handle non-finite values.
Results may differ from a plain program's by a relative error of at most 0.017.
Values may be sent and summed in bfloat16 or wider, within the bound.
A program may use at most 128 MiB of HBM per device.

v0:
```python
import jax
import jax.numpy as jnp
from jax import lax
from jax.sharding import PartitionSpec as P

HEAD_DIM = 64
L = 512


def rms_norm(values, gain):
    wide = values.astype(jnp.float32)
    square = jnp.mean(wide * wide, axis=-1, keepdims=True)
    return (wide * lax.rsqrt(square + 1e-05) * gain[None, :]).astype(jnp.bfloat16)


def rotate(values, times):
    half = values.shape[-1] // 2
    freq = 10000.0 ** (-jnp.arange(half, dtype=jnp.float32) / half)
    angle = times.astype(jnp.float32)[:, None] * freq[None, :]
    cosine = jnp.cos(angle)[:, None, :]
    sine = jnp.sin(angle)[:, None, :]
    first = values[..., :half]
    second = values[..., half:]
    return jnp.concatenate(
        [first * cosine - second * sine, first * sine + second * cosine], axis=-1
    )


def rotated(raw, times):
    row_total, local_width = raw.shape
    turned = rotate(raw.reshape(row_total, local_width // HEAD_DIM, HEAD_DIM), times)
    return turned.reshape(row_total, local_width).astype(jnp.bfloat16)


def attend(queries, keys_rot, values, samples, variates, bias):
    row_total, local_width = queries.shape
    heads_here = local_width // HEAD_DIM
    count = row_total // L

    def one_sequence(args):
        qs, ks, vs, sample_row, variate_row = args
        scores = jnp.einsum(
            "qhd,khd->hqk", qs, ks, preferred_element_type=jnp.float32
        ) * HEAD_DIM ** (-0.5)
        same = variate_row[:, None] == variate_row[None, :]
        scores = scores + jnp.where(same[None], bias[0][:, None, None], bias[1][:, None, None])
        scores = jnp.where((sample_row[:, None] == sample_row[None, :])[None], scores, -1e30)
        top = jnp.max(scores, axis=2, keepdims=True)
        expo = jnp.exp(scores - top)
        weights = (expo / jnp.sum(expo, axis=2, keepdims=True)).astype(jnp.bfloat16)
        return jnp.einsum("hqk,khd->qhd", weights, vs, preferred_element_type=jnp.float32).astype(
            jnp.bfloat16
        )

    shape = (count, L, heads_here, HEAD_DIM)
    result = lax.map(
        one_sequence,
        (
            queries.reshape(shape),
            keys_rot.reshape(shape),
            values.reshape(shape),
            samples.reshape(count, L),
            variates.reshape(count, L),
        ),
    )
    return result.reshape(row_total, local_width)


def local(
    tokens,
    norm_gain,
    qkv_weight,
    out_weight,
    variate_bias,
    ffn_weight,
    down_weight,
    sample_ids,
    variate_ids,
    time_ids,
):
    heads_here = qkv_weight.shape[2] // HEAD_DIM
    head_start = lax.axis_index("mp") * heads_here
    bias_local = lax.dynamic_slice_in_dim(variate_bias, head_start, heads_here, 1)
    first_normed = rms_norm(tokens, norm_gain[0])
    wide_columns = lax.all_gather(qkv_weight, "mp", axis=2, tiled=True)
    columns = first_normed
    projected = jnp.einsum(
        "rc,jcd->jrd",
        columns,
        lax.all_gather(wide_columns, "dp", axis=1, tiled=True),
        preferred_element_type=jnp.float32,
    )
    queries = rotated(projected[0], time_ids)
    keys_rot = rotated(projected[1], time_ids)
    values = projected[2].astype(jnp.bfloat16)
    grouped = lax.all_to_all(
        jnp.stack([queries, keys_rot, values]), "mp", split_axis=2, concat_axis=1, tiled=True
    )
    gathered_ids = (
        lax.all_gather(sample_ids, "mp", axis=0, tiled=True),
        lax.all_gather(variate_ids, "mp", axis=0, tiled=True),
    )
    attended = attend(
        grouped[0], grouped[1], grouped[2], gathered_ids[0], gathered_ids[1], bias_local
    )
    back_rows = lax.all_to_all(attended, "mp", split_axis=0, concat_axis=1, tiled=True)
    out_rows = lax.all_gather(out_weight, "mp", axis=0, tiled=True)
    mixed = jnp.dot(
        back_rows,
        lax.all_gather(out_rows, "dp", axis=1, tiled=True),
        preferred_element_type=jnp.float32,
    )
    residual = (tokens.astype(jnp.float32) + mixed).astype(jnp.bfloat16)
    second_normed = rms_norm(residual, norm_gain[1])
    ffn_columns = lax.all_gather(ffn_weight, "mp", axis=2, tiled=True)
    columns = second_normed
    gate_up = jnp.einsum(
        "rc,jcf->jrf",
        columns,
        lax.all_gather(ffn_columns, "dp", axis=1, tiled=True),
        preferred_element_type=jnp.float32,
    )
    hidden = (jax.nn.silu(gate_up[0]) * gate_up[1]).astype(jnp.bfloat16)
    down_full = lax.all_gather(down_weight, "mp", axis=0, tiled=True)
    feed = jnp.dot(
        hidden,
        lax.all_gather(down_full, "dp", axis=1, tiled=True),
        preferred_element_type=jnp.float32,
    )
    return (residual.astype(jnp.float32) + feed).astype(jnp.bfloat16)


def solution(mesh):
    return jax.shard_map(
        local,
        mesh=mesh,
        in_specs=(
            P(("dp", "mp"), None),
            P(),
            P(None, "dp", "mp"),
            P("mp", "dp"),
            P(),
            P(None, "dp", "mp"),
            P("mp", "dp"),
            P(("dp", "mp")),
            P(("dp", "mp")),
            P(("dp", "mp")),
        ),
        out_specs=P(("dp", "mp"), None),
        check_vma=False,
    )
```

profile of v0, /device:TPU:0, one launch (start us, length us, event | category | flops | bytes accessed | tf_op | source)
XLA Modules:
  0.0 358.3 jit_solution(14907393396261247635)
XLA Ops:
  6.5 2.2 copy.40
  8.8 27.7 %all_gather.30 = bf16[3,128,1024]{2,1,0:T(8,128)(2,1)} all-gather(bf16[3,128,256]{2,1,0:T(8,128)(2,1)} %param.14), channel_id=1, replica_groups=mesh['dp'=8,'mp'=4] {'mp'}, dimensions={2}, use_global_device_ids=true | all-gather | bytes 983040 | tf_op jit(solution)/shard_map/all_gather | solution.py:85
  36.6 18.9 %all_gather.34 = bf16[1024,128]{1,0:T(8,128)(2,1)} all-gather(bf16[256,128]{1,0:T(8,128)(2,1)} %param.15), channel_id=1, replica_groups=mesh['dp'=8,'mp'=4] {'mp'}, dimensions={0}, use_global_device_ids=true | all-gather | bytes 327680 | tf_op jit(solution)/shard_map/all_gather | solution.py:107
  56.8 4.9 %copy.41 = bf16[2,128,2816]{2,1,0:T(8,128)(2,1)} copy(bf16[2,128,2816]{1,0,2:T(2,128)(2,1)} %all-gather.12.cloned.1.call-done) | data formatting | bytes 2883584 | tf_op jit(solution)/shard_map/all_gather | solution.py:115
  62.3 41.2 %all-gather.8.cloned.1.call-done = bf16[3,1024,1024]{2,1,0:T(8,128)(2,1)} async-done(((bf16[3,128,1024]{2,1,0:T(8,128)(2,1)}), bf16[3,1024,1024]{2,1,0:T(8,128)(2,1)}) %all-gather.8.cloned.1.call-update) | async-done | bytes 6291472 | tf_op jit(solution)/shard_map/all_gather | solution.py:90
  103.5 5.7 %convolution_bitcast_fusion.1 = f32[3,512,1024]{2,1,0:T(8,128)S(1)} fusion(bf16[3,1024,1024]{2,1,0:T(8,128)(2,1)} %all-gather.8.cloned.1.call-done, bf16[512,1024]{1,0:T(8,128)(2,1)S(1)} %copy-done.2, f32[1024]{0:T(1024)S(1)} %bitcast.128, f32[512]{0:T(512)S(1)} %add_rsqrt_fusion.1), kind=kOutput, calls=%fused_computation.54 | convolution fusion | flops 3223322624 | bytes 13637632 | tf_op jit(solution)/shard_map/rc,jcd->jrd/dot_general | solution.py:87
  110.4 2.4 fusion.80
  112.8 2.0 copy.34
  114.8 2.9 copy.35
  117.7 2.3 subtract_convert_fusion.1
  122.8 2.5 pad_maximum_fusion
  125.3 5.7 %copy.38 = bf16[3,512,1024]{1,0,2:T(4,128)(2,1)} copy(bf16[3,512,1024]{2,1,0:T(8,128)(2,1)S(1)} %pad_maximum_fusion) | data formatting | bytes 6291456 | tf_op jit(solution)/shard_map/stack | solution.py:97
  131.0 5.0 %all-to-all-start = ((bf16[3,512,1024]{1,0,2:T(4,128)(2,1)}), bf16[3,512,1024]{1,0,2:T(4,128)(2,1)}, u32[]{:S(2)}, u32[]{:S(2)}) async-start(bf16[3,512,1024]{1,0,2:T(4,128)(2,1)} %copy.38), calls=%async_computation | async-start | bytes 8388608 | tf_op jit(solution)/shard_map/all_to_all | solution.py:96
  136.1 106.7 %all_gather.38 = bf16[2816,128]{1,0:T(8,128)(2,1)} all-gather(bf16[704,128]{1,0:T(8,128)(2,1)S(1)} %copy-done.4), channel_id=1, replica_groups=mesh['dp'=8,'mp'=4] {'mp'}, dimensions={0}, use_global_device_ids=true | all-gather | bytes 901120 | tf_op jit(solution)/shard_map/all_gather | solution.py:124
  242.9 11.9 %all-gather.1 = s32[4,1,512]{2,1,0:T(1,128)S(1)} all-gather(s32[1,1,512]{2,1,0:T(1,128)S(1)} %bitcast.129), channel_id=1, replica_groups=mesh['dp'=8,'mp'=4] {'mp'}, dimensions={0}, use_global_device_ids=true | all-gather | bytes 10240 | tf_op jit(solution)/shard_map/all_gather | solution.py:101
  254.8 12.1 %all-gather = s32[4,1,512]{2,1,0:T(1,128)S(1)} all-gather(s32[1,1,512]{2,1,0:T(1,128)S(1)} %bitcast.130), channel_id=1, replica_groups=mesh['dp'=8,'mp'=4] {'mp'}, dimensions={0}, use_global_device_ids=true | all-gather | bytes 10240 | tf_op jit(solution)/shard_map/all_gather | solution.py:100
  267.0 3.2 copy.39
  270.2 1.5 fusion.81
  271.7 31.2 %while.10 = (s32[]{:T(128)}, bf16[4,512,4,64]{1,3,2,0:T(8,128)(2,1)}, bf16[4,512,4,64]{1,3,2,0:T(8,128)(2,1)}, s32[4,512]{1,0:T(4,128)S(1)}, bf16[4,512,4,64]{1,...) while((s32[]{:T(128)}, ...), condition=%wide.region_4.5_spmd, body=%wide.region_1.4_spmd.sunk | while | flops 416943104 | bytes 3179681 | solution.py:56
  272.2 3.0 fusion.100
  275.2 4.3 %fusion.101 = bf16[4,512,4,64]{1,3,2,0:T(8,128)(2,1)} fusion(bf16[4,512,4,64]{1,3,2,0:T(8,128)(2,1)} %get-tuple-element.154, s32[]{:T(128)} %get-tuple-element.153, f32[4,512]{1,0:T(4,128)S(1)} %fusion.100, bf16[4,512,4,64]{1,3,2,0:T(8,128)(2,1)} %get-tuple-element.164, f32[4]{0:T(128)S(1)} %get-tuple-element.140, f32[4]{0:T(128)S(1)} %get-tuple-element.141, ...), kind=kOutput, calls=%fused_computation.14.clone.1 | convolution fusion | flops 275909120 | bytes 1584128 | tf_op jit(solution)/shard_map/while/body/eval_jaxpr/hqk,khd->qhd/dot_general | solution.py:51
  280.0 3.0 fusion.100
  283.0 4.3 %fusion.101 = bf16[4,512,4,64]{1,3,2,0:T(8,128)(2,1)} fusion(bf16[4,512,4,64]{1,3,2,0:T(8,128)(2,1)} %get-tuple-element.154, s32[]{:T(128)} %get-tuple-element.153, f32[4,512]{1,0:T(4,128)S(1)} %fusion.100, bf16[4,512,4,64]{1,3,2,0:T(8,128)(2,1)} %get-tuple-element.164, f32[4]{0:T(128)S(1)} %get-tuple-element.140, f32[4]{0:T(128)S(1)} %get-tuple-element.141, ...), kind=kOutput, calls=%fused_computation.14.clone.1 | convolution fusion | flops 275909120 | bytes 1584128 | tf_op jit(solution)/shard_map/while/body/eval_jaxpr/hqk,khd->qhd/dot_general | solution.py:51
  287.8 3.0 fusion.100
  290.8 4.3 %fusion.101 = bf16[4,512,4,64]{1,3,2,0:T(8,128)(2,1)} fusion(bf16[4,512,4,64]{1,3,2,0:T(8,128)(2,1)} %get-tuple-element.154, s32[]{:T(128)} %get-tuple-element.153, f32[4,512]{1,0:T(4,128)S(1)} %fusion.100, bf16[4,512,4,64]{1,3,2,0:T(8,128)(2,1)} %get-tuple-element.164, f32[4]{0:T(128)S(1)} %get-tuple-element.140, f32[4]{0:T(128)S(1)} %get-tuple-element.141, ...), kind=kOutput, calls=%fused_computation.14.clone.1 | convolution fusion | flops 275909120 | bytes 1584128 | tf_op jit(solution)/shard_map/while/body/eval_jaxpr/hqk,khd->qhd/dot_general | solution.py:51
  295.6 3.0 fusion.100
  298.6 4.3 %fusion.101 = bf16[4,512,4,64]{1,3,2,0:T(8,128)(2,1)} fusion(bf16[4,512,4,64]{1,3,2,0:T(8,128)(2,1)} %get-tuple-element.154, s32[]{:T(128)} %get-tuple-element.153, f32[4,512]{1,0:T(4,128)S(1)} %fusion.100, bf16[4,512,4,64]{1,3,2,0:T(8,128)(2,1)} %get-tuple-element.164, f32[4]{0:T(128)S(1)} %get-tuple-element.140, f32[4]{0:T(128)S(1)} %get-tuple-element.141, ...), kind=kOutput, calls=%fused_computation.14.clone.1 | convolution fusion | flops 275909120 | bytes 1584128 | tf_op jit(solution)/shard_map/while/body/eval_jaxpr/hqk,khd->qhd/dot_general | solution.py:51
  302.9 3.7 %all-to-all-start.1 = ((bf16[4,512,256]{1,2,0:T(8,128)(2,1)}), bf16[4,512,256]{1,2,0:T(8,128)(2,1)S(1)}, u32[]{:S(2)}, u32[]{:S(2)}) async-start(bf16[4,512,256]{1,2,0:T(8,128)(2,1)} %bitcast.24), calls=%async_computation.1 | async-start | bytes 2097152 | tf_op jit(solution)/shard_map/all_to_all | solution.py:106
  306.7 18.6 %all-to-all-done.1 = bf16[4,512,256]{1,2,0:T(8,128)(2,1)S(1)} async-done(((bf16[4,512,256]{1,2,0:T(8,128)(2,1)}), bf16[4,512,256]{1,2,0:T(8,128)(2,1)S(1)}, u32[]{:S(2)}, u32[]{:S(2)}) %all-to-all-start.1) | async-done | bytes 1048608 | tf_op jit(solution)/shard_map/all_to_all | solution.py:106
  325.3 3.0 fusion.60
  328.3 13.2 %convolution_bitcast_fusion = f32[2,512,2816]{2,1,0:T(8,128)} fusion(bf16[2,1024,2816]{2,1,0:T(8,128)(2,1)} %all-gather.14.cloned.1.call-done, bf16[512,1024]{1,0:T(8,128)(2,1)S(1)} %get-tuple-element.84, f32[1024]{0:T(1024)S(1)} %bitcast.125, f32[512]{0:T(512)S(1)} %add_rsqrt_fusion), kind=kOutput, calls=%fused_computation.41 | convolution fusion | flops 5907677184 | bytes 24123392 | tf_op jit(solution)/shard_map/rc,jcf->jrf/dot_general | solution.py:117
  341.6 10.2 %fusion.63 = bf16[512,1024]{1,0:T(8,128)(2,1)} fusion(bf16[512,1024]{1,0:T(8,128)(2,1)S(1)} %get-tuple-element.84, bf16[2816,1024]{1,0:T(8,128)(2,1)} %all-gather.16.cloned.1.call-done, f32[2,512,2816]{2,1,0:T(8,128)} %convolution_bitcast_fusion), kind=kOutput, calls=%fused_computation.62 | convolution fusion | flops 2963013632 | bytes 19398656 | tf_op jit(solution)/shard_map/dot_general | solution.py:125
  (64 shorter events, 8.0 us)
Async XLA Ops:
  6.5 260.4 %copy-start = (f32[2,16]{1,0:T(2,128)S(1)}, f32[2,16]{1,0:T(2,128)}, u32[]{:S(2)}) copy-start(f32[2,16]{1,0:T(2,128)} %param.16) | copy-start | bytes 388
  6.5 55.1 %copy-start.8 = (s32[512]{0:T(512)S(1)}, s32[512]{0:T(512)}, u32[]{:S(2)}) copy-start(s32[512]{0:T(512)} %param.21) | copy-start | bytes 6148
  6.5 55.2 %copy-start.2 = (bf16[512,1024]{1,0:T(8,128)(2,1)S(1)}, bf16[512,1024]{1,0:T(8,128)(2,1)}, u32[]{:S(2)}) copy-start(bf16[512,1024]{1,0:T(8,128)(2,1)} %param.12) | copy-start | bytes 3145732
  6.5 50.2 %all-gather.12.cloned.1.call-start = ((), (), s32[]{:S(2)}) async-start(), calls=%async_computation.4 | async-start | bytes 1802240 | tf_op jit(solution)/shard_map/all_gather | solution.py:115
  8.7 53.3 %copy-start.5 = (f32[2,1024]{1,0:T(2,128)S(1)}, f32[2,1024]{1,0:T(2,128)}, u32[]{:S(2)}) copy-start(f32[2,1024]{1,0:T(2,128)} %param.13) | copy-start | bytes 24580
  8.8 94.8 %all-gather.8.cloned.1.call-start = ((), (), s32[]{:S(2)}) async-start(), calls=%async_computation.2 | async-start | bytes 7077888 | tf_op jit(solution)/shard_map/all_gather | solution.py:90
  36.5 270.2 %all-gather.10.cloned.1.call-start = ((), (), s32[]{:S(2)}) async-start(), calls=%async_computation.3 | async-start | bytes 2359296 | tf_op jit(solution)/shard_map/all_gather | solution.py:110
  55.5 272.8 %all-gather.14.cloned.1.call-start = ((), (), s32[]{:S(2)}) async-start(), calls=%async_computation.5 | async-start | bytes 12976128 | tf_op jit(solution)/shard_map/all_gather | solution.py:120
  131.0 5.1 %copy-start.4 = (bf16[704,128]{1,0:T(8,128)(2,1)S(1)}, bf16[704,128]{1,0:T(8,128)(2,1)}, u32[]{:S(2)}) copy-start(bf16[704,128]{1,0:T(8,128)(2,1)} %param.18) | copy-start | bytes 540676
  131.0 111.8 %copy-start.6 = (s32[512]{0:T(512)S(1)}, s32[512]{0:T(512)}, u32[]{:S(2)}) copy-start(s32[512]{0:T(512)} %param.20) | copy-start | bytes 6148
  131.0 123.8 %copy-start.7 = (s32[512]{0:T(512)S(1)}, s32[512]{0:T(512)}, u32[]{:S(2)}) copy-start(s32[512]{0:T(512)} %param.19) | copy-start | bytes 6148
  131.0 136.0 %all-to-all-start = ((bf16[3,512,1024]{1,0,2:T(4,128)(2,1)}), bf16[3,512,1024]{1,0,2:T(4,128)(2,1)}, u32[]{:S(2)}, u32[]{:S(2)}) async-start(bf16[3,512,1024]{1,0,2:T(4,128)(2,1)} %copy.38), calls=%async_computation | async-start | bytes 8388608 | tf_op jit(solution)/shard_map/all_to_all | solution.py:96
  136.0 205.6 %all-gather.16.cloned.1.call-start = ((), (), s32[]{:S(2)}) async-start(), calls=%async_computation.6 | async-start | bytes 6488064 | tf_op jit(solution)/shard_map/all_gather | solution.py:127
  271.7 53.6 %copy-start.3 = (bf16[512,1024]{1,0:T(8,128)(2,1)S(1)}, bf16[512,1024]{1,0:T(8,128)(2,1)}, u32[]{:S(2)}) copy-start(bf16[512,1024]{1,0:T(8,128)(2,1)} %param.12) | copy-start | bytes 3145732
  302.9 22.3 %all-to-all-start.1 = ((bf16[4,512,256]{1,2,0:T(8,128)(2,1)}), bf16[4,512,256]{1,2,0:T(8,128)(2,1)S(1)}, u32[]{:S(2)}, u32[]{:S(2)}) async-start(bf16[4,512,256]{1,2,0:T(8,128)(2,1)} %bitcast.24), calls=%async_computation.1 | async-start | bytes 2097152 | tf_op jit(solution)/shard_map/all_to_all | solution.py:106
  341.6 10.2 %copy-start.1 = (f32[2,16]{1,0:T(2,128)S(1)}, f32[2,16]{1,0:T(2,128)}, u32[]{:S(2)}) copy-start(f32[2,16]{1,0:T(2,128)} %param.16) | copy-start | bytes 388
Sparse Core Ops, SparseCore 0:
  8.9 47.8 all-gather.11
  58.7 44.7 all-gather.7
  105.4 28.0 all-gather.9
  135.3 67.5 all-gather.13
  243.0 44.4 all-gather.15
where the time goes:
time: 359 us; the launch traced here: 358 us
  blocking collectives  177 us (49%)
  matrix products  61.5 us (17%)
  waiting for transfers between devices  61.1 us (17%)
  local copies, waits for them, and re-layouts  28.7 us (8%)
  between operations  13.3 us (4%)
  starting transfers between devices  8.9 us (2%)
  other arithmetic  7.24 us (2%)
    all_gather x1, blocking collectives, local(): down_full = lax.all_gather(down_weight, 'mp', axis=0, tiled=True)  107 us
    all_gather x1, waiting for transfers between devices, local(): lax.all_gather(wide_columns, 'dp', axis=1, tiled=True)  41.2 us
    all_gather x1, blocking collectives, local(): wide_columns = lax.all_gather(qkv_weight, 'mp', axis=2, tiled=True)  27.7 us
    all_gather x1, blocking collectives, local(): out_rows = lax.all_gather(out_weight, 'mp', axis=0, tiled=True)  18.9 us
    all_to_all x1, waiting for transfers between devices, local(): lax.all_to_all(attended, 'mp', split_axis=0, concat_axis=1, tiled=True)  18.6 us
    dot_general x4, matrix products, one_sequence(): jnp.einsum('hqk,khd->qhd', weights, vs, preferred_element_type=jnp.float32)  17.2 us
    dot_general x1, matrix products, local(): jnp.einsum('rc,jcf->jrf', columns, lax.all_gather(ffn_columns, 'dp', axis...  13.2 us
    sub x4, matrix products, one_sequence(): expo = jnp.exp(scores - top)  12.1 us
  transfers between devices with their start and end apart: 7, of which 3 were waited for; matrix products, arithmetic and copies ran while one was open for 24% of the time, Pallas kernels for 0%

commit v1 on v0

--- a/solution.py
+++ b/solution.py
@@ -1,10 +1,27 @@
+import functools
 import jax
 import jax.numpy as jnp
 from jax import lax
 from jax.sharding import PartitionSpec as P
+from jax.lax import axis_index, axis_size, ppermute
 
 HEAD_DIM = 64
 L = 512
+
+
+def link_chains_for(base_x, mesh_dim, out_dim):
+    slots = axis_size(mesh_dim)
+    spare = [(c - 1, c) for c in range(1, slots)] + [(slots - 1, 0)]
+    v_next = base_x
+    chunks = [v_next]
+    for _ in range(slots - 1):
+        v_next = ppermute(v_next, axis_name=mesh_dim, perm=spare)
+        chunks += [v_next]
+    field_out = jnp.concatenate([*reversed(chunks)], out_dim)
+    return jnp.roll(field_out, (axis_index(mesh_dim) + 1) * v_next.shape[out_dim], out_dim)
+
+
+work_strings = functools.partial(link_chains_for, mesh_dim="mp", out_dim=2)
 
 
 def rms_norm(values, gain):
@@ -82,7 +99,7 @@
     head_start = lax.axis_index("mp") * heads_here
     bias_local = lax.dynamic_slice_in_dim(variate_bias, head_start, heads_here, 1)
     first_normed = rms_norm(tokens, norm_gain[0])
-    wide_columns = lax.all_gather(qkv_weight, "mp", axis=2, tiled=True)
+    wide_columns = work_strings(qkv_weight)
     columns = first_normed
     projected = jnp.einsum(
         "rc,jcd->jrd",

time: 359 us -> 344 us (0.958)
  blocking collectives: 177 us -> 149 us
  waiting for transfers between devices: 61.1 us -> 84.1 us
  local copies, waits for them, and re-layouts: 28.7 us -> 19.4 us
  other arithmetic: 7.24 us -> 3.55 us
    ppermute x0 -> x3, waiting for transfers between devices: none -> 33 us  [link_chains_for(): v_next = ppermute(v_next, axis_name=mesh_dim, perm=spare)]
    all_gather x1 -> x0, blocking collectives: 27.7 us -> none  [local(): wide_columns = lax.all_gather(qkv_weight, 'mp', axis=2, tiled=True)]
    all_gather x1, waiting for transfers between devices: 41.2 us -> 32.2 us  [local(): lax.all_gather(wide_columns, 'dp', axis=1, tiled=True)]
    slice x2 -> x1, local copies, waits for them, and re-layouts: 4.39 us -> 0.44 us  [local(): queries = rotated(projected[0], time_ids)]
  transfers between devices with their start and end apart: 7 -> 10, of which waited for: 3 -> 5; matrix products, arithmetic and copies ran while one was open for 24% -> 21% of each run, Pallas kernels for 0% -> 0%
where the time goes in v1:
time: 344 us; the launch traced here: 343 us
  blocking collectives  149 us (43%)
  waiting for transfers between devices  84.1 us (24%)
  matrix products  61.6 us (18%)
  local copies, waits for them, and re-layouts  19.4 us (6%)
  between operations  13.4 us (4%)
  starting transfers between devices  11.8 us (3%)
  other arithmetic  3.55 us (1%)
    all_gather x1, blocking collectives, local(): down_full = lax.all_gather(down_weight, 'mp', axis=0, tiled=True)  107 us
    ppermute x3, waiting for transfers between devices, link_chains_for(): v_next = ppermute(v_next, axis_name=mesh_dim, perm=spare)  33 us
    all_gather x1, waiting for transfers between devices, local(): lax.all_gather(wide_columns, 'dp', axis=1, tiled=True)  32.2 us
    all_to_all x1, waiting for transfers between devices, local(): lax.all_to_all(attended, 'mp', split_axis=0, concat_axis=1, tiled=True)  18.8 us
    all_gather x1, blocking collectives, local(): out_rows = lax.all_gather(out_weight, 'mp', axis=0, tiled=True)  18.2 us
    dot_general x4, matrix products, one_sequence(): jnp.einsum('hqk,khd->qhd', weights, vs, preferred_element_type=jnp.float32)  17.2 us
    dot_general x1, matrix products, local(): jnp.einsum('rc,jcf->jrf', columns, lax.all_gather(ffn_columns, 'dp', axis...  13.2 us
    sub x4, matrix products, one_sequence(): expo = jnp.exp(scores - top)  12.1 us
  transfers between devices with their start and end apart: 10, of which 5 were waited for; matrix products, arithmetic and copies ran while one was open for 21% of the time, Pallas kernels for 0%

profile of v1, /device:TPU:0, one launch (start us, length us, event | category | flops | bytes accessed | tf_op | source)
XLA Modules:
  0.0 343.0 jit_solution(10446594139064830189)
XLA Ops:
  6.5 2.1 copy.29
  8.7 1.1 copy.24
  9.8 3.1 collective-permute-start
  12.9 6.9 %collective-permute-done = bf16[3,128,256]{1,2,0:T(8,128)(2,1)S(1)} collective-permute-done((bf16[3,128,256]{1,2,0:T(8,128)(2,1)S(1)}, bf16[3,128,256]{1,2,0:T(8,128)(2,1)S(1)}, u32[]{:S(2)}, u32[]{:S(2)}) %collective-permute-start) | collective-permute-done | bytes 196640 | tf_op jit(solution)/shard_map/ppermute | solution.py:18
  19.9 13.0 %collective-permute-done.1 = bf16[3,128,256]{1,2,0:T(8,128)(2,1)S(1)} collective-permute-done((bf16[3,128,256]{1,2,0:T(8,128)(2,1)S(1)}, bf16[3,128,256]{1,2,0:T(8,128)(2,1)S(1)}, u32[]{:S(2)}, u32[]{:S(2)}) %collective-permute-start.1) | collective-permute-done | bytes 196640 | tf_op jit(solution)/shard_map/ppermute | solution.py:18
  32.9 13.0 %collective-permute-done.2 = bf16[3,128,256]{1,2,0:T(8,128)(2,1)S(1)} collective-permute-done((bf16[3,128,256]{1,2,0:T(8,128)(2,1)S(1)}, bf16[3,128,256]{1,2,0:T(8,128)(2,1)S(1)}, u32[]{:S(2)}, u32[]{:S(2)}) %collective-permute-start.2) | collective-permute-done | bytes 196640 | tf_op jit(solution)/shard_map/ppermute | solution.py:18
  46.2 0.9 constant_dynamic-slice_fusion.3
  47.2 18.2 %all_gather.30 = bf16[1024,128]{1,0:T(8,128)(2,1)} all-gather(bf16[256,128]{1,0:T(8,128)(2,1)S(1)} %copy-done.4), channel_id=1, replica_groups=mesh['dp'=8,'mp'=4] {'mp'}, dimensions={0}, use_global_device_ids=true | all-gather | bytes 327680 | tf_op jit(solution)/shard_map/all_gather | solution.py:124
  65.6 5.0 %copy.30 = bf16[2,128,2816]{2,1,0:T(8,128)(2,1)} copy(bf16[2,128,2816]{1,0,2:T(2,128)(2,1)} %all-gather.12.cloned.1.call-done) | data formatting | bytes 2883584 | tf_op jit(solution)/shard_map/all_gather | solution.py:132
  71.2 32.2 %all-gather.8.cloned.1.call-done = bf16[3,1024,1024]{1,2,0:T(8,128)(2,1)} async-done(((bf16[3,128,1024]{1,2,0:T(8,128)(2,1)}), bf16[3,1024,1024]{1,2,0:T(8,128)(2,1)}) %all-gather.8.cloned.1.call-update) | async-done | bytes 6291472 | tf_op jit(solution)/shard_map/all_gather | solution.py:107
  103.4 5.8 %convolution_bitcast_fusion.1 = f32[3,512,1024]{1,2,0:T(8,128)S(1)} fusion(bf16[3,1024,1024]{1,2,0:T(8,128)(2,1)} %all-gather.8.cloned.1.call-done, bf16[512,1024]{1,0:T(8,128)(2,1)S(1)} %copy-done.2, f32[1024]{0:T(1024)S(1)} %bitcast.128, f32[512]{0:T(512)S(1)} %add_rsqrt_fusion.1), kind=kOutput, calls=%fused_computation.54 | convolution fusion | flops 3223322624 | bytes 13637632 | tf_op jit(solution)/shard_map/rc,jcd->jrd/dot_general | solution.py:104
  111.0 4.6 %copy.27 = bf16[3,512,1024]{1,0,2:T(4,128)(2,1)} copy(bf16[3,512,1024]{1,2,0:T(8,128)(2,1)S(1)} %pad_maximum_fusion) | data formatting | bytes 6291456 | tf_op jit(solution)/shard_map/stack | solution.py:114
  115.7 5.0 %all-to-all-start = ((bf16[3,512,1024]{1,0,2:T(4,128)(2,1)}), bf16[3,512,1024]{1,0,2:T(4,128)(2,1)}, u32[]{:S(2)}, u32[]{:S(2)}) async-start(bf16[3,512,1024]{1,0,2:T(4,128)(2,1)} %copy.27), calls=%async_computation | async-start | bytes 8388608 | tf_op jit(solution)/shard_map/all_to_all | solution.py:113
  120.7 106.7 %all_gather.34 = bf16[2816,128]{1,0:T(8,128)(2,1)} all-gather(bf16[704,128]{1,0:T(8,128)(2,1)S(1)} %copy-done.3), channel_id=1, replica_groups=mesh['dp'=8,'mp'=4] {'mp'}, dimensions={0}, use_global_device_ids=true | all-gather | bytes 901120 | tf_op jit(solution)/shard_map/all_gather | solution.py:141
  227.5 11.9 %all-gather.1 = s32[4,1,512]{2,1,0:T(1,128)S(1)} all-gather(s32[1,1,512]{2,1,0:T(1,128)S(1)} %bitcast.129), channel_id=1, replica_groups=mesh['dp'=8,'mp'=4] {'mp'}, dimensions={0}, use_global_device_ids=true | all-gather | bytes 10240 | tf_op jit(solution)/shard_map/all_gather | solution.py:118
  239.5 12.1 %all-gather = s32[4,1,512]{2,1,0:T(1,128)S(1)} all-gather(s32[1,1,512]{2,1,0:T(1,128)S(1)} %bitcast.130), channel_id=1, replica_groups=mesh['dp'=8,'mp'=4] {'mp'}, dimensions={0}, use_global_device_ids=true | all-gather | bytes 10240 | tf_op jit(solution)/shard_map/all_gather | solution.py:117
  251.6 3.2 copy.28
  254.8 1.6 fusion.81
  256.4 31.2 %while.10 = (s32[]{:T(128)}, bf16[4,512,4,64]{1,3,2,0:T(8,128)(2,1)}, bf16[4,512,4,64]{1,3,2,0:T(8,128)(2,1)}, s32[4,512]{1,0:T(4,128)S(1)}, bf16[4,512,4,64]{1,...) while((s32[]{:T(128)}, ...), condition=%wide.region_4.5_spmd, body=%wide.region_1.4_spmd.sunk | while | flops 416943104 | bytes 3179681 | solution.py:73
  256.8 3.0 fusion.100
  259.9 4.3 %fusion.101 = bf16[4,512,4,64]{1,3,2,0:T(8,128)(2,1)} fusion(bf16[4,512,4,64]{1,3,2,0:T(8,128)(2,1)} %get-tuple-element.154, s32[]{:T(128)} %get-tuple-element.153, f32[4,512]{1,0:T(4,128)S(1)} %fusion.100, bf16[4,512,4,64]{1,3,2,0:T(8,128)(2,1)} %get-tuple-element.164, f32[4]{0:T(128)S(1)} %get-tuple-element.140, f32[4]{0:T(128)S(1)} %get-tuple-element.141, ...), kind=kOutput, calls=%fused_computation.14.clone.1 | convolution fusion | flops 275909120 | bytes 1584128 | tf_op jit(solution)/shard_map/while/body/eval_jaxpr/hqk,khd->qhd/dot_general | solution.py:68
  264.6 3.0 fusion.100
  267.7 4.3 %fusion.101 = bf16[4,512,4,64]{1,3,2,0:T(8,128)(2,1)} fusion(bf16[4,512,4,64]{1,3,2,0:T(8,128)(2,1)} %get-tuple-element.154, s32[]{:T(128)} %get-tuple-element.153, f32[4,512]{1,0:T(4,128)S(1)} %fusion.100, bf16[4,512,4,64]{1,3,2,0:T(8,128)(2,1)} %get-tuple-element.164, f32[4]{0:T(128)S(1)} %get-tuple-element.140, f32[4]{0:T(128)S(1)} %get-tuple-element.141, ...), kind=kOutput, calls=%fused_computation.14.clone.1 | convolution fusion | flops 275909120 | bytes 1584128 | tf_op jit(solution)/shard_map/while/body/eval_jaxpr/hqk,khd->qhd/dot_general | solution.py:68
  272.4 3.0 fusion.100
  275.5 4.3 %fusion.101 = bf16[4,512,4,64]{1,3,2,0:T(8,128)(2,1)} fusion(bf16[4,512,4,64]{1,3,2,0:T(8,128)(2,1)} %get-tuple-element.154, s32[]{:T(128)} %get-tuple-element.153, f32[4,512]{1,0:T(4,128)S(1)} %fusion.100, bf16[4,512,4,64]{1,3,2,0:T(8,128)(2,1)} %get-tuple-element.164, f32[4]{0:T(128)S(1)} %get-tuple-element.140, f32[4]{0:T(128)S(1)} %get-tuple-element.141, ...), kind=kOutput, calls=%fused_computation.14.clone.1 | convolution fusion | flops 275909120 | bytes 1584128 | tf_op jit(solution)/shard_map/while/body/eval_jaxpr/hqk,khd->qhd/dot_general | solution.py:68
  280.2 3.0 fusion.100
  283.3 4.3 %fusion.101 = bf16[4,512,4,64]{1,3,2,0:T(8,128)(2,1)} fusion(bf16[4,512,4,64]{1,3,2,0:T(8,128)(2,1)} %get-tuple-element.154, s32[]{:T(128)} %get-tuple-element.153, f32[4,512]{1,0:T(4,128)S(1)} %fusion.100, bf16[4,512,4,64]{1,3,2,0:T(8,128)(2,1)} %get-tuple-element.164, f32[4]{0:T(128)S(1)} %get-tuple-element.140, f32[4]{0:T(128)S(1)} %get-tuple-element.141, ...), kind=kOutput, calls=%fused_computation.14.clone.1 | convolution fusion | flops 275909120 | bytes 1584128 | tf_op jit(solution)/shard_map/while/body/eval_jaxpr/hqk,khd->qhd/dot_general | solution.py:68
  287.6 3.5 %all-to-all-start.1 = ((bf16[4,512,256]{1,2,0:T(8,128)(2,1)}), bf16[4,512,256]{1,2,0:T(8,128)(2,1)S(1)}, u32[]{:S(2)}, u32[]{:S(2)}) async-start(bf16[4,512,256]{1,2,0:T(8,128)(2,1)} %bitcast.24), calls=%async_computation.1 | async-start | bytes 2097152 | tf_op jit(solution)/shard_map/all_to_all | solution.py:123
  291.1 18.8 %all-to-all-done.1 = bf16[4,512,256]{1,2,0:T(8,128)(2,1)S(1)} async-done(((bf16[4,512,256]{1,2,0:T(8,128)(2,1)}), bf16[4,512,256]{1,2,0:T(8,128)(2,1)S(1)}, u32[]{:S(2)}, u32[]{:S(2)}) %all-to-all-start.1) | async-done | bytes 1048608 | tf_op jit(solution)/shard_map/all_to_all | solution.py:123
  309.9 3.0 fusion.60
  313.0 13.2 %convolution_bitcast_fusion = f32[2,512,2816]{2,1,0:T(8,128)} fusion(bf16[2,1024,2816]{2,1,0:T(8,128)(2,1)} %all-gather.14.cloned.1.call-done, bf16[512,1024]{1,0:T(8,128)(2,1)S(1)} %get-tuple-element.84, f32[1024]{0:T(1024)S(1)} %bitcast.125, f32[512]{0:T(512)S(1)} %add_rsqrt_fusion), kind=kOutput, calls=%fused_computation.41 | convolution fusion | flops 5907677184 | bytes 24123392 | tf_op jit(solution)/shard_map/rc,jcf->jrf/dot_general | solution.py:134
  326.2 10.2 %fusion.63 = bf16[512,1024]{1,0:T(8,128)(2,1)} fusion(bf16[512,1024]{1,0:T(8,128)(2,1)S(1)} %get-tuple-element.84, bf16[2816,1024]{1,0:T(8,128)(2,1)} %all-gather.16.cloned.1.call-done, f32[2,512,2816]{2,1,0:T(8,128)} %convolution_bitcast_fusion), kind=kOutput, calls=%fused_computation.62 | convolution fusion | flops 2963013632 | bytes 19398656 | tf_op jit(solution)/shard_map/dot_general | solution.py:142
  (75 shorter events, 4.8 us)
Async XLA Ops:
  6.5 245.0 %copy-start = (f32[2,16]{1,0:T(2,128)S(1)}, f32[2,16]{1,0:T(2,128)}, u32[]{:S(2)}) copy-start(f32[2,16]{1,0:T(2,128)} %param.16) | copy-start | bytes 388
  6.5 59.0 %all-gather.12.cloned.1.call-start = ((), (), s32[]{:S(2)}) async-start(), calls=%async_computation.4 | async-start | bytes 1802240 | tf_op jit(solution)/shard_map/all_gather | solution.py:132
  8.7 38.5 %copy-start.4 = (bf16[256,128]{1,0:T(8,128)(2,1)S(1)}, bf16[256,128]{1,0:T(8,128)(2,1)}, u32[]{:S(2)}) copy-start(bf16[256,128]{1,0:T(8,128)(2,1)} %param.15) | copy-start | bytes 196612
  8.7 94.7 %all-gather.8.cloned.1.call-start = ((), (), s32[]{:S(2)}) async-start(), calls=%async_computation.2 | async-start | bytes 7077888 | tf_op jit(solution)/shard_map/all_gather | solution.py:107
  9.8 10.0 %collective-permute-start = (bf16[3,128,256]{1,2,0:T(8,128)(2,1)S(1)}, bf16[3,128,256]{1,2,0:T(8,128)(2,1)S(1)}, u32[]{:S(2)}, u32[]{:S(2)}) collective-permute-start(bf16[3,128,256]{1,2,0:T(8,128)(2,1)S(1)} %copy.24), channel_id=1, source_target_pairs={{0,1},{1,2},{2,3},{3,0},{4,5},{5,6},{6,7},{7,4},{8,9},{9,10},{10,1... | collective-permute-start | bytes 589832 | tf_op jit(solution)/shard_map/ppermute | solution.py:18
  19.9 13.0 %collective-permute-start.1 = (bf16[3,128,256]{1,2,0:T(8,128)(2,1)S(1)}, bf16[3,128,256]{1,2,0:T(8,128)(2,1)S(1)}, u32[]{:S(2)}, u32[]{:S(2)}) collective-permute-start(bf16[3,128,256]{1,2,0:T(8,128)(2,1)S(1)} %collective-permute-done), channel_id=1, source_target_pairs={{0,1},{1,2},{2,3},{3,0},{4,5},{5,6},{6,7},{7,4},{8,9},{9,10},{10,1... | collective-permute-start | bytes 589832 | tf_op jit(solution)/shard_map/ppermute | solution.py:18
  32.9 13.0 %collective-permute-start.2 = (bf16[3,128,256]{1,2,0:T(8,128)(2,1)S(1)}, bf16[3,128,256]{1,2,0:T(8,128)(2,1)S(1)}, u32[]{:S(2)}, u32[]{:S(2)}) collective-permute-start(bf16[3,128,256]{1,2,0:T(8,128)(2,1)S(1)} %collective-permute-done.1), channel_id=1, source_target_pairs={{0,1},{1,2},{2,3},{3,0},{4,5},{5,6},{6,7},{7,4},{8,9},{9,10},{10,1... | collective-permute-start | bytes 589832 | tf_op jit(solution)/shard_map/ppermute | solution.py:18
  47.1 23.4 %copy-start.8 = (s32[512]{0:T(512)S(1)}, s32[512]{0:T(512)}, u32[]{:S(2)}) copy-start(s32[512]{0:T(512)} %param.21) | copy-start | bytes 6148
  47.1 23.5 %copy-start.2 = (bf16[512,1024]{1,0:T(8,128)(2,1)S(1)}, bf16[512,1024]{1,0:T(8,128)(2,1)}, u32[]{:S(2)}) copy-start(bf16[512,1024]{1,0:T(8,128)(2,1)} %param.12) | copy-start | bytes 3145732
  47.2 244.0 %all-gather.10.cloned.1.call-start = ((), (), s32[]{:S(2)}) async-start(), calls=%async_computation.3 | async-start | bytes 2359296 | tf_op jit(solution)/shard_map/all_gather | solution.py:127
  65.4 5.4 %copy-start.5 = (f32[2,1024]{1,0:T(2,128)S(1)}, f32[2,1024]{1,0:T(2,128)}, u32[]{:S(2)}) copy-start(f32[2,1024]{1,0:T(2,128)} %param.13) | copy-start | bytes 24580
  65.5 247.5 %all-gather.14.cloned.1.call-start = ((), (), s32[]{:S(2)}) async-start(), calls=%async_computation.5 | async-start | bytes 12976128 | tf_op jit(solution)/shard_map/all_gather | solution.py:137
  115.7 5.1 %copy-start.3 = (bf16[704,128]{1,0:T(8,128)(2,1)S(1)}, bf16[704,128]{1,0:T(8,128)(2,1)}, u32[]{:S(2)}) copy-start(bf16[704,128]{1,0:T(8,128)(2,1)} %param.18) | copy-start | bytes 540676
  115.7 111.8 %copy-start.6 = (s32[512]{0:T(512)S(1)}, s32[512]{0:T(512)}, u32[]{:S(2)}) copy-start(s32[512]{0:T(512)} %param.20) | copy-start | bytes 6148
  115.7 123.8 %copy-start.7 = (s32[512]{0:T(512)S(1)}, s32[512]{0:T(512)}, u32[]{:S(2)}) copy-start(s32[512]{0:T(512)} %param.19) | copy-start | bytes 6148
  115.7 136.0 %all-to-all-start = ((bf16[3,512,1024]{1,0,2:T(4,128)(2,1)}), bf16[3,512,1024]{1,0,2:T(4,128)(2,1)}, u32[]{:S(2)}, u32[]{:S(2)}) async-start(bf16[3,512,1024]{1,0,2:T(4,128)(2,1)} %copy.27), calls=%async_computation | async-start | bytes 8388608 | tf_op jit(solution)/shard_map/all_to_all | solution.py:113
  120.7 205.6 %all-gather.16.cloned.1.call-start = ((), (), s32[]{:S(2)}) async-start(), calls=%async_computation.6 | async-start | bytes 6488064 | tf_op jit(solution)/shard_map/all_gather | solution.py:144
  287.6 22.4 %all-to-all-start.1 = ((bf16[4,512,256]{1,2,0:T(8,128)(2,1)}), bf16[4,512,256]{1,2,0:T(8,128)(2,1)S(1)}, u32[]{:S(2)}, u32[]{:S(2)}) async-start(bf16[4,512,256]{1,2,0:T(8,128)(2,1)} %bitcast.24), calls=%async_computation.1 | async-start | bytes 2097152 | tf_op jit(solution)/shard_map/all_to_all | solution.py:123
  326.2 10.2 %copy-start.1 = (f32[2,16]{1,0:T(2,128)S(1)}, f32[2,16]{1,0:T(2,128)}, u32[]{:S(2)}) copy-start(f32[2,16]{1,0:T(2,128)} %param.16) | copy-start | bytes 388
Sparse Core Ops, SparseCore 0:
  8.9 47.4 all-gather.11
  58.3 45.0 all-gather.7
  105.3 28.0 all-gather.9
  135.2 67.5 all-gather.13
  227.6 44.5 all-gather.15
